TPU v7x, 32 devices: a whole 2x2x4 slice. The times are simulated.
32 devices in a mesh: row: 4 (over y, x), col: 8 (over z, core).
Axes of the slice: x: 2, y: 2, z: 4, core: 2. Of those that a mesh axis runs over, the one named last changes fastest.
Arguments:
- values: bfloat16 [4096, 4096], P('row', 'col'), may hold values from 0.0001296997 to 0.12988281
- tile_mask: int32 [32, 32], P('row', 'col'), may hold values 0 or 1
- keep_mask: int32 [32, 32], P('row', 'col'), may hold values 0 or 1
- thr_index: int32 [4096], P('col'), may hold values from 0 to 9
Outputs:
- expanded: bfloat16 [4096, 4096], P('row', 'col')
All inputs are finite; a program needn't handle non-finite values. No bound on the sum of `tile_mask` or of `keep_mask` on one device may be relied on, other than what follows from the above.
Results may differ from a plain program's by a relative error of at most 0.0004.
Values may be sent and summed in bfloat16 or wider, within the bound.
A program may use at most 64 MiB of HBM per device.

v0:
```python
import jax
import jax.numpy as jnp
from jax import lax
from jax.sharding import PartitionSpec as P

TB = 128


def on_device(values, tile_mask, keep_mask, thr_index):
    row_count, col_count = values.shape
    row_tiles = row_count // TB
    col_tiles = col_count // TB
    matrix = (
        values.reshape(row_tiles, TB, col_tiles, TB)
        * tile_mask[:, None, :, None].astype(jnp.bfloat16)
    ).reshape(row_count, col_count)
    kept_cells = jnp.broadcast_to(
        keep_mask[:, None, :, None].astype(jnp.float32), (row_tiles, TB, col_tiles, TB)
    ).reshape(row_count, col_count)
    order_all = row_count * lax.axis_size("row")
    thresholds = 0.125 * thr_index.astype(jnp.float32)
    col_panel = lax.all_gather(matrix, "row", axis=0, tiled=True)
    product = jnp.dot(
        lax.all_gather(matrix, "col", axis=1, tiled=True),
        col_panel,
        preferred_element_type=jnp.float32,
    )
    outputs = []
    for phase_idx in range(col_tiles):
        lo_col = phase_idx * TB
        part_prod = product[:, lo_col : lo_col + TB]
        col_means = lax.psum(jnp.sum(part_prod, axis=0), "row") / order_all
        pruned = (
            jnp.maximum(part_prod - thresholds[lo_col : lo_col + TB] * col_means, 0.0)
            * kept_cells[:, lo_col : lo_col + TB]
        )
        col_totals = lax.psum(jnp.sum(pruned, axis=0), "row") / order_all
        outputs.append(pruned / jnp.maximum(col_totals, 0.1))
    result = jnp.concatenate(outputs, axis=1)
    return result.astype(jnp.bfloat16)


def solution(mesh):
    return jax.shard_map(
        on_device,
        mesh=mesh,
        in_specs=(P("row", "col"), P("row", "col"), P("row", "col"), P("col")),
        out_specs=P("row", "col"),
        check_vma=False,
    )
```

profile of v0, /device:TPU:0, one launch (start us, length us, event | category | flops | bytes accessed | tf_op | source)
XLA Modules:
  0.0 188.3 jit_solution(8773886451617511830)
XLA Ops:
  6.5 0.0 all-gather.5.cloned.1.call-start
  6.5 0.7 convert_element_type.12
  7.2 0.1 copy.5
  7.3 0.3 mul.41
  7.7 0.0 copy-start.1
  7.7 2.3 %bitcast_multiply_fusion = bf16[1024,512]{1,0:T(8,128)(2,1)} fusion(bf16[1024,512]{1,0:T(8,128)(2,1)} %param.4, bf16[128,8,4,128]{3,2,1,0:T(4,128)(2,1)S(1)} %bitcast.14), kind=kLoop, calls=%fused_computation.1 | loop fusion | flops 524288 | bytes 3145728 | tf_op jit(solution)/shard_map/mul | solution.py:14
  10.0 0.0 all-gather.5.cloned.1.call-update
  10.0 0.0 all-gather.3.cloned.1.call-start
  10.1 0.7 all-gather.3.cloned.1.call-update
  10.8 0.1 copy.6
  10.9 0.3 broadcast_in_dim.2
  11.2 0.0 copy-start.2
  11.3 0.2 copy.11
  11.4 0.5 copy-done.2
  11.9 53.6 %all-gather.5.cloned.1.call-done = bf16[4096,512]{1,0:T(8,128)(2,1)} async-done(((bf16[1024,512]{1,0:T(8,128)(2,1)}), bf16[4096,512]{1,0:T(8,128)(2,1)}) %all-gather.5.cloned.1.call-update) | async-done | bytes 4194320 | tf_op jit(solution)/shard_map/all_gather | solution.py:22
  65.5 83.7 %all-gather.3.cloned.1.call-done = bf16[1024,4096]{1,0:T(8,128)(2,1)} async-done(((bf16[1024,512]{1,0:T(8,128)(2,1)}), bf16[1024,4096]{1,0:T(8,128)(2,1)}) %all-gather.3.cloned.1.call-update) | async-done | bytes 8388624 | tf_op jit(solution)/shard_map/all_gather | solution.py:24
  149.2 8.1 %fusion.4 = f32[1024,512]{1,0:T(8,128)S(1)} fusion(bf16[1024,4096]{1,0:T(8,128)(2,1)} %all-gather.3.cloned.1.call-done, bf16[4096,512]{1,0:T(8,128)(2,1)} %all-gather.5.cloned.1.call-done), kind=kOutput, calls=%fused_computation.28 | convolution fusion | flops 4294967296 | bytes 14680064 | tf_op jit(solution)/shard_map/dot_general | solution.py:23
  157.3 1.3 copy-done
  158.7 0.2 slice_reduce_fusion.3
  158.8 9.8 %all-reduce.1 = (f32[128]{0:T(128)S(1)}, f32[128]{0:T(128)S(1)}, f32[128]{0:T(128)S(1)}, f32[128]{0:T(128)S(1)}) all-reduce(f32[128]{0:T(128)S(1)} %get-tuple-element.9, f32[128]{0:T(128)S(1)} %get-tuple-element.10, f32[128]{0:T(128)S(1)} %get-tuple-element.11, f32[128]{0:T(128)S(1)} %get-tuple-element.12), channel_id=1, replica_groups=mesh['row'=4,'col'=8] {'row'}, use_global_device_ids=true, to_apply=%region_1.0 | all-reduce | flops 512 | bytes 4096 | tf_op jit(solution)/shard_map/psum | solution.py:32
  168.7 1.8 fusion
  170.5 8.0 %all-reduce = (f32[128]{0:T(128)S(1)}, f32[128]{0:T(128)S(1)}, f32[128]{0:T(128)S(1)}, f32[128]{0:T(128)S(1)}) all-reduce(f32[128]{0:T(128)S(1)} %get-tuple-element.6, f32[128]{0:T(128)S(1)} %get-tuple-element.7, f32[128]{0:T(128)S(1)} %get-tuple-element.8, f32[128]{0:T(128)S(1)} %get-tuple-element.5), channel_id=1, replica_groups=mesh['row'=4,'col'=8] {'row'}, use_global_device_ids=true, to_apply=%region_15.0 | all-reduce | flops 512 | bytes 4096 | tf_op jit(solution)/shard_map/psum | solution.py:37
  178.5 1.9 %divide_convert_fusion.3 = (bf16[1024,128]{1,0:T(8,128)(2,1)S(1)}, bf16[1024,128]{1,0:T(8,128)(2,1)S(1)}, bf16[1024,128]{1,0:T(8,128)(2,1)S(1)}, bf16[1024,128]{1,0:T(8,128)(2,1)S(1)}) fusion(f32[128]{0:T(128)S(1)} %get-tuple-element.32, f32[1024,512]{1,0:T(8,128)S(1)} %bitcast.12, f32[128]{0:T(128)S(1)} %get-tuple-element.28, f32[1024,512]{1,0:T(8,128)} %copy-done, ...), kind=kLoop, calls=%fused_computation.10 | loop fusion | flops 2621440 | bytes 5246976 | tf_op jit(solution)/shard_map/convert
  180.4 1.1 pad_maximum_fusion
  (7 shorter events, 0.0 us)
Async XLA Ops:
  6.5 59.0 %all-gather.5.cloned.1.call-start = ((), (), s32[]{:S(2)}) async-start(), calls=%async_computation.1 | async-start | bytes 5242880 | tf_op jit(solution)/shard_map/all_gather | solution.py:22
  7.7 3.1 %copy-start.1 = (s32[8,4]{0,1:T(4,128)S(1)}, s32[8,4]{0,1:T(4,128)}, u32[]{:S(2)}) copy-start(s32[8,4]{0,1:T(4,128)} %param.6) | copy-start | bytes 388
  10.0 139.1 %all-gather.3.cloned.1.call-start = ((), (), s32[]{:S(2)}) async-start(), calls=%async_computation | async-start | bytes 9437184 | tf_op jit(solution)/shard_map/all_gather | solution.py:24
  11.2 0.7 copy-start.2
  157.3 1.4 copy-start
Sparse Core Ops, SparseCore 0:
  10.2 55.2 all-gather.4
  67.1 82.0 all-gather.2
where the time goes:
time: 189 us; the launch traced here: 188 us
  waiting for transfers between devices  138 us (73%)
  blocking collectives  17.8 us (9%)
  between operations  13.5 us (7%)
  matrix products  8.14 us (4%)
  other arithmetic  8.02 us (4%)
  local copies, waits for them, and re-layouts  2.87 us (2%)
    all_gather x1, waiting for transfers between devices, on_device(): lax.all_gather(matrix, 'col', axis=1, tiled=True)  83.7 us
    all_gather x1, waiting for transfers between devices, on_device(): col_panel = lax.all_gather(matrix, 'row', axis=0, tiled=True)  53.6 us
    psum x1, blocking collectives, on_device(): col_means = lax.psum(jnp.sum(part_prod, axis=0), 'row') / order_all  9.85 us
    dot_general x1, matrix products, on_device(): jnp.dot(lax.all_gather(matrix, 'col', axis=1, tiled=True), col_panel, pre...  8.14 us
    psum x1, blocking collectives, on_device(): col_totals = lax.psum(jnp.sum(pruned, axis=0), 'row') / order_all  7.98 us
  transfers between devices with their start and end apart: 2, of which 2 were waited for; matrix products, arithmetic and copies ran while one was open for 0% of the time, Pallas kernels for 0%

commit v1 on v0

v1 whole, which is shorter than its diff:
```python
import functools

import jax
import jax.numpy as jnp
from jax import lax
from jax.experimental import pallas as pl
from jax.experimental.pallas import tpu as pltpu
from jax.sharding import PartitionSpec as P

TB = 128
CORES = 2
CHUNKS = 4


def snake(index, width):
    line, spot = index // width, index % width
    return line * width + spot + (line % 2) * (width - 1 - 2 * spot)


def kernel(
    row_dev, col_dev, width, chunks, order,
    v_ref, tile_ref, keep_ref, thr_ref, out_ref,
    row_panel, col_panel, acc, sums,
    line_send, line_recv, pair_send, pair_recv, ring_send, ring_recv, sum_send, sum_recv,
):
    rows, cols = v_ref.shape
    step_rows = rows // chunks
    chips = col_dev // CORES
    half = row_dev // 2
    me_row, me_col = lax.axis_index("row"), lax.axis_index("col")
    z, core = me_col // CORES, me_col % CORES
    pos = snake(me_row, width)

    def ring_device(offset):
        return snake((pos + offset + row_dev) % row_dev, width)

    barrier = pltpu.get_barrier_semaphore()
    pl.semaphore_signal(barrier, inc=1, device_id={"col": z * CORES + 1 - core})
    for d in range(1, row_dev):
        pl.semaphore_signal(barrier, inc=1, device_id={"row": (me_row + d) % row_dev})

    @pl.when(z > 0)
    def _():
        pl.semaphore_signal(barrier, inc=1, device_id={"col": me_col - CORES})

    @pl.when(z < chips - 1)
    def _():
        pl.semaphore_signal(barrier, inc=1, device_id={"col": me_col + CORES})

    for a in range(rows // TB):
        for b in range(cols // TB):
            r, c = slice(a * TB, (a + 1) * TB), slice(b * TB, (b + 1) * TB)
            scale = tile_ref[a, b].astype(jnp.float32)
            tile = (v_ref[r, c].astype(jnp.float32) * scale).astype(jnp.bfloat16)
            row_panel[me_col, r, c] = tile
            col_panel[pl.ds(pl.multiple_of(me_row * rows + a * TB, TB), TB), c] = tile

    pl.semaphore_wait(
        barrier, row_dev + (z > 0).astype(jnp.int32) + (z < chips - 1).astype(jnp.int32)
    )

    def row_part(block, q):
        return row_panel.at[block, pl.ds(q * step_rows, step_rows)]

    def line_copy(zi, q, to_right):
        part = row_part(zi * CORES + core, q)
        return pltpu.make_async_remote_copy(
            src_ref=part, dst_ref=part,
            send_sem=line_send.at[to_right, zi, q], recv_sem=line_recv.at[zi, q],
            device_id={"col": me_col + (CORES if to_right else -CORES)},
        )

    def pair_copy(zi, q, lane):
        part = row_part(zi * CORES + lane, q)
        return pltpu.make_async_remote_copy(
            src_ref=part, dst_ref=part,
            send_sem=pair_send.at[zi, q], recv_sem=pair_recv.at[zi, q],
            device_id={"col": z * CORES + 1 - core},
        )

    def ring_copy(owner, q, to_right):
        start = pl.multiple_of(owner * rows + q * step_rows, step_rows)
        part = col_panel.at[pl.ds(start, step_rows)]
        return pltpu.make_async_remote_copy(
            src_ref=part, dst_ref=part,
            send_sem=ring_send.at[to_right, owner, q], recv_sem=ring_recv.at[owner, q],
            device_id={"row": ring_device(1 if to_right else -1)},
        )

    def on_ring(d, q, to_right):
        if d < half:
            return True
        return d == half and (q < chunks // 2) == bool(to_right)

    def relay(zi, q, to_right, wait):
        if wait:
            line_copy(zi, q, to_right).wait_recv()
        go = (z < chips - 1) if to_right else (z > 0)

        @pl.when(go)
        def _():
            line_copy(zi, q, to_right).start()

    for q in range(chunks):
        for to_right in (1, 0):
            relay(z, q, to_right, False)
            if on_ring(1, q, to_right):
                ring_copy(me_row, q, to_right).start()
        pair_copy(z, q, core).start()

    def step(t, q):
        for to_right in (1, 0):
            valid = (z >= t) if to_right else (z + t < chips)
            zi = z - t if to_right else z + t
            if t < chips:
                @pl.when(valid)
                def _():
                    relay(zi, q, to_right, True)
                    pair_copy(zi, q, core).start()
            if on_ring(t, q, to_right):
                owner = ring_device(-t if to_right else t)
                ring_copy(owner, q, to_right).wait_recv()
                if on_ring(t + 1, q, to_right):
                    ring_copy(owner, q, to_right).start()

    def compute(zi, q, first=False):
        spot = pl.ds(pl.multiple_of(q * step_rows, step_rows), step_rows)
        total = None
        for lane in range(CORES):
            block = zi * CORES + lane
            inner = pl.ds(pl.multiple_of(block * cols, cols), cols)
            term = jnp.dot(
                row_panel[block, spot], col_panel[inner], preferred_element_type=jnp.float32
            )
            total = term if total is None else total + term
        if first:
            acc[spot] = total
        else:
            acc[spot] += total

    def take(zi, q, first=False):
        pair_copy(zi, q, 1 - core).wait_recv()
        compute(zi, q, first)

    def sides(t):
        return ((z >= t, z - t), (z + t < chips, z + t))

    def bulk(upto):
        @pl.loop(0, chunks)
        def _(q):
            take(z, q, True)
            for t in range(1, min(upto, chips - 1) + 1):
                for valid, zi in sides(t):
                    @pl.when(valid)
                    def _():
                        take(zi, q)

    if half == 0:
        bulk(0)
    for t in range(1, max(chips - 1, half) + 1):
        for q in range(chunks):
            step(t, q)
            if t > half:
                for valid, zi in sides(t):
                    @pl.when(valid)
                    def _():
                        take(zi, q)
        if t == half:
            bulk(t)

    def all_sum(phase, part):
        sums[phase, 0] = part

        def sum_copy(d):
            return pltpu.make_async_remote_copy(
                src_ref=sums.at[phase, 0], dst_ref=sums.at[phase, d],
                send_sem=sum_send.at[phase, d], recv_sem=sum_recv.at[phase, d],
                device_id={"row": (me_row + d) % row_dev},
            )

        for d in range(1, row_dev):
            sum_copy(d).start()
        total = part
        for d in range(1, row_dev):
            sum_copy(d).wait()
            total = total + sums[phase, d]
        return total

    cut = (
        0.125 * thr_ref[...].astype(jnp.float32)
        * (all_sum(0, jnp.sum(acc[...], axis=0, keepdims=True)) / order)
    )
    parts = []
    for b in range(cols // TB):
        c = slice(b * TB, (b + 1) * TB)
        part = jnp.zeros((1, TB), jnp.float32)
        for a in range(rows // TB):
            r = slice(a * TB, (a + 1) * TB)
            pruned = jnp.maximum(acc[r, c] - cut[:, c], 0.0) * keep_ref[a, b].astype(jnp.float32)
            acc[r, c] = pruned
            part += jnp.sum(pruned, axis=0, keepdims=True)
        parts.append(part)
    totals = all_sum(1, jnp.concatenate(parts, axis=1)) / order
    out_ref[...] = (acc[...] * (1.0 / jnp.maximum(totals, 0.1))).astype(jnp.bfloat16)

    for q in range(chunks):
        for zi in range(chips):
            pair_copy(zi, q, core).wait_send()

            @pl.when((z < chips - 1) & (z >= zi))
            def _():
                line_copy(zi, q, 1).wait_send()

            @pl.when((z > 0) & (z <= zi))
            def _():
                line_copy(zi, q, 0).wait_send()
        for d in range(0, half):
            for to_right in (1, 0):
                if on_ring(d + 1, q, to_right):
                    owner = ring_device(-d if to_right else d)
                    ring_copy(owner, q, to_right).wait_send()


def on_device(values, tile_mask, keep_mask, thr_index, *, row_dev, col_dev):
    rows, cols = values.shape
    width = max(w for w in range(1, row_dev + 1) if row_dev % w == 0 and w * w <= row_dev)
    chips = col_dev // CORES
    dma = pltpu.SemaphoreType.DMA
    return pl.pallas_call(
        functools.partial(kernel, row_dev, col_dev, width, CHUNKS, rows * row_dev),
        out_shape=jax.ShapeDtypeStruct((rows, cols), jnp.bfloat16),
        in_specs=[
            pl.BlockSpec(memory_space=pltpu.VMEM),
            pl.BlockSpec(memory_space=pltpu.SMEM),
            pl.BlockSpec(memory_space=pltpu.SMEM),
            pl.BlockSpec(memory_space=pltpu.VMEM),
        ],
        out_specs=pl.BlockSpec(memory_space=pltpu.VMEM),
        scratch_shapes=[
            pltpu.VMEM((col_dev, rows, cols), jnp.bfloat16),
            pltpu.VMEM((row_dev * rows, cols), jnp.bfloat16),
            pltpu.VMEM((rows, cols), jnp.float32),
            pltpu.VMEM((2, row_dev, 1, cols), jnp.float32),
            dma((2, chips, CHUNKS)),
            dma((chips, CHUNKS)),
            dma((chips, CHUNKS)),
            dma((chips, CHUNKS)),
            dma((2, row_dev, CHUNKS)),
            dma((row_dev, CHUNKS)),
            dma((2, row_dev)),
            dma((2, row_dev)),
        ],
        compiler_params=pltpu.CompilerParams(
            collective_id=0, has_side_effects=True, vmem_limit_bytes=60 * 1024 * 1024
        ),
    )(values, tile_mask, keep_mask, thr_index.reshape(1, cols))


def solution(mesh):
    return jax.shard_map(
        functools.partial(on_device, row_dev=mesh.shape["row"], col_dev=mesh.shape["col"]),
        mesh=mesh,
        in_specs=(P("row", "col"), P("row", "col"), P("row", "col"), P("col")),
        out_specs=P("row", "col"),
        check_vma=False,
    )
```

time: 189 us -> 88.7 us (0.47)
  waiting for transfers between devices: 138 us -> 0 us
  Pallas kernels: 0 us -> 84.1 us
  blocking collectives: 17.8 us -> 0 us
  between operations: 13.5 us -> 0.01 us
  matrix products: 8.14 us -> 0 us
  other arithmetic: 8.02 us -> 0 us
    all_gather x2 -> x0, waiting for transfers between devices: 137 us -> none  [the longest x1 83.7 us: on_device(): lax.all_gather(matrix, 'col', axis=1, tiled=True)]
    pallas_call x0 -> x1, Pallas kernels: none -> 84.1 us  [on_device(): pl.pallas_call(functools.partial(kernel, row_dev, col_dev, width, CHUNKS,...]
    psum x2 -> x0, blocking collectives: 17.8 us -> none  [the longest x1 9.85 us: on_device(): col_means = lax.psum(jnp.sum(part_prod, axis=0), 'row') / order_all]
    dot_general x1 -> x0, matrix products: 8.14 us -> none  [on_device(): jnp.dot(lax.all_gather(matrix, 'col', axis=1, tiled=True), col_panel, pre...]
    mul x3 -> x0, other arithmetic: 2.36 us -> none  [the longest x1 2.34 us: on_device(): values.reshape(row_tiles, TB, col_tiles, TB)]
    unnamed x7 -> x5, local copies, waits for them, and re-layouts: 2.02 us -> 4.3 us
    reduce_sum x2 -> x0, other arithmetic: 1.98 us -> none  [the longest x1 1.83 us: on_device(): col_totals = lax.psum(jnp.sum(pruned, axis=0), 'row') / order_all]
    another operation x1 -> x0, other arithmetic: 1.9 us -> none
  transfers between devices with their start and end apart: 2 -> 0, of which waited for: 2 -> 0; matrix products, arithmetic and copies ran while one was open for 0% -> 0% of each run, Pallas kernels for 0% -> 0%
where the time goes in v1:
time: 88.7 us; the launch traced here: 88.5 us
  Pallas kernels  84.1 us (95%)
  local copies, waits for them, and re-layouts  4.3 us (5%)
    pallas_call x1, Pallas kernels, on_device(): pl.pallas_call(functools.partial(kernel, row_dev, col_dev, width, CHUNKS,...  84.1 us
    unnamed x5, local copies, waits for them, and re-layouts  4.3 us

profile of v1, /device:TPU:0, one launch (start us, length us, event | category | flops | bytes accessed | tf_op | source)
XLA Modules:
  0.0 88.5 jit_solution(9041084207039743854)
XLA Ops:
  0.0 0.0 copy-start
  0.0 1.4 %copy.5.tile_ref = s32[8,4]{1,0:T(8,128)} copy(s32[8,4]{0,1:T(4,128)} %param.5) | data formatting | bytes 256 | tf_op args[1]
  1.4 0.0 copy-done
  1.4 0.7 copy.6.keep_ref
  2.0 84.1 %shard_map.46 = bf16[1024,512]{1,0:T(8,128)(2,1)} custom-call(bf16[1024,512]{1,0:T(8,128)(2,1)} %v_ref.1, s32[8,4]{1,0:T(8,128)} %copy.5.tile_ref, s32[8,4]{1,0:T(8,128)} %copy.6.keep_ref, s32[1,512]{1,0:T(1,128)} %bitcast.1), custom_call_target="tpu_custom_call" | custom-call | tf_op jit(solution)/shard_map/pallas_call | solution.py:229
  86.2 2.3 %copy.8 = bf16[1024,512]{1,0:T(8,128)(2,1)} copy(bf16[1024,512]{1,0:T(8,128)(2,1)} %shard_map.46) | data formatting | bytes 2097152
Async XLA Ops:
  0.0 1.4 %copy-start = (s32[8,4]{0,1:T(4,128)S(1)}, s32[8,4]{0,1:T(4,128)}, u32[]{:S(2)}) copy-start(s32[8,4]{0,1:T(4,128)} %param.6) | copy-start | bytes 388

commit v2 on v1

--- a/solution.py
+++ b/solution.py
@@ -9,7 +9,7 @@
 
 TB = 128
 CORES = 2
-CHUNKS = 4
+CHUNKS = 8
 
 
 def snake(index, width):
@@ -19,9 +19,10 @@
 
 def kernel(
     row_dev, col_dev, width, chunks, order,
-    v_ref, tile_ref, keep_ref, thr_ref, out_ref,
-    row_panel, col_panel, acc, sums,
-    line_send, line_recv, pair_send, pair_recv, ring_send, ring_recv, sum_send, sum_recv,
+    v_ref, tile_ref, keep_ref, thr_ref, pruned_ref, totals_ref,
+    row_panel, col_panel, acc, sums, stats,
+    line_send, line_recv, pair_send, pair_recv, ring_send, ring_recv,
+    sum_send, sum_recv, stat_send, stat_recv, out_sem,
 ):
     rows, cols = v_ref.shape
     step_rows = rows // chunks
@@ -35,29 +36,22 @@
         return snake((pos + offset + row_dev) % row_dev, width)
 
     barrier = pltpu.get_barrier_semaphore()
-    pl.semaphore_signal(barrier, inc=1, device_id={"col": z * CORES + 1 - core})
     for d in range(1, row_dev):
         pl.semaphore_signal(barrier, inc=1, device_id={"row": (me_row + d) % row_dev})
-
-    @pl.when(z > 0)
-    def _():
-        pl.semaphore_signal(barrier, inc=1, device_id={"col": me_col - CORES})
-
-    @pl.when(z < chips - 1)
-    def _():
-        pl.semaphore_signal(barrier, inc=1, device_id={"col": me_col + CORES})
-
+    for d in range(1, col_dev):
+        pl.semaphore_signal(barrier, inc=1, device_id={"col": (me_col + d) % col_dev})
+
+    stored = tile_ref[...].astype(jnp.float32)
+    kept = keep_ref[...].astype(jnp.float32)
     for a in range(rows // TB):
         for b in range(cols // TB):
             r, c = slice(a * TB, (a + 1) * TB), slice(b * TB, (b + 1) * TB)
-            scale = tile_ref[a, b].astype(jnp.float32)
+            scale = jnp.broadcast_to(stored[b : b + 1, a : a + 1], (TB, TB))
             tile = (v_ref[r, c].astype(jnp.float32) * scale).astype(jnp.bfloat16)
             row_panel[me_col, r, c] = tile
             col_panel[pl.ds(pl.multiple_of(me_row * rows + a * TB, TB), TB), c] = tile
 
-    pl.semaphore_wait(
-        barrier, row_dev + (z > 0).astype(jnp.int32) + (z < chips - 1).astype(jnp.int32)
-    )
+    pl.semaphore_wait(barrier, row_dev + col_dev - 2)
 
     def row_part(block, q):
         return row_panel.at[block, pl.ds(q * step_rows, step_rows)]
@@ -108,7 +102,7 @@
                 ring_copy(me_row, q, to_right).start()
         pair_copy(z, q, core).start()
 
-    def step(t, q):
+    def line_step(t, q):
         for to_right in (1, 0):
             valid = (z >= t) if to_right else (z + t < chips)
             zi = z - t if to_right else z + t
@@ -117,11 +111,49 @@
                 def _():
                     relay(zi, q, to_right, True)
                     pair_copy(zi, q, core).start()
+
+    def ring_step(t, q):
+        for to_right in (1, 0):
             if on_ring(t, q, to_right):
                 owner = ring_device(-t if to_right else t)
                 ring_copy(owner, q, to_right).wait_recv()
                 if on_ring(t + 1, q, to_right):
                     ring_copy(owner, q, to_right).start()
+
+    def stat_copy(d):
+        return pltpu.make_async_remote_copy(
+            src_ref=stats.at[0], dst_ref=stats.at[d],
+            send_sem=stat_send.at[d], recv_sem=stat_recv.at[d],
+            device_id={"col": (me_col + d) % col_dev},
+        )
+
+    def send_stats():
+        total = jnp.zeros((1, cols), jnp.float32)
+        for i in range(row_dev):
+            block = col_panel[i * rows : (i + 1) * rows].astype(jnp.float32)
+            total += jnp.sum(block, axis=0, keepdims=True)
+        stats[0] = total
+        for d in range(1, col_dev):
+            stat_copy(d).start()
+
+    def product_sums():
+        total = jnp.zeros((1, cols), jnp.float32)
+        for d in range(col_dev):
+            if d:
+                stat_copy(d).wait()
+            block = (me_col - d + col_dev) % col_dev
+            inner = pl.ds(pl.multiple_of(block * cols, cols), cols)
+            rest, terms = stats[d], []
+            for _ in range(3):
+                term = rest.astype(jnp.bfloat16).astype(jnp.float32)
+                rest = rest - term
+                terms.append(jnp.broadcast_to(term, (8, cols)))
+            spread = jnp.dot(
+                jnp.concatenate(terms, axis=0).astype(jnp.bfloat16), col_panel[inner],
+                preferred_element_type=jnp.float32,
+            )
+            total += spread[16:17] + spread[8:9] + spread[0:1]
+        return total
 
     def compute(zi, q, first=False):
         spot = pl.ds(pl.multiple_of(q * step_rows, step_rows), step_rows)
@@ -155,53 +187,79 @@
                     def _():
                         take(zi, q)
 
+    def out_copy(q):
+        spot = pl.ds(q * step_rows, step_rows)
+        return pltpu.make_async_copy(acc.at[spot], pruned_ref.at[spot], out_sem.at[q])
+
+    def prune(q, cut):
+        parts = []
+        for b in range(cols // TB):
+            c = slice(b * TB, (b + 1) * TB)
+            part = jnp.zeros((1, TB), jnp.float32)
+            for lo in range(q * step_rows, (q + 1) * step_rows, min(step_rows, TB)):
+                r = slice(lo, lo + min(step_rows, TB))
+                keep = jnp.broadcast_to(kept[b : b + 1, lo // TB : lo // TB + 1], (r.stop - lo, TB))
+                pruned = jnp.maximum(acc[r, c] - cut[:, c], 0.0) * keep
+                acc[r, c] = pruned
+                part += jnp.sum(pruned, axis=0, keepdims=True)
+            parts.append(part)
+        return jnp.concatenate(parts, axis=1)
+
+    def cuts():
+        return 0.125 * thr_ref[...].astype(jnp.float32) * (product_sums() / order)
+
+    part = jnp.zeros((1, cols), jnp.float32)
+    last = max(chips - 1, half)
     if half == 0:
+        send_stats()
         bulk(0)
-    for t in range(1, max(chips - 1, half) + 1):
+    for t in range(1, last + 1):
+        if t == half:
+            for q in range(chunks):
+                ring_step(t, q)
+            send_stats()
+            for q in range(chunks):
+                line_step(t, q)
+            bulk(t)
+        else:
+            if t == last and t > half:
+                cut = cuts()
+            for q in range(chunks):
+                line_step(t, q)
+                if t < half:
+                    ring_step(t, q)
+                else:
+                    for valid, zi in sides(t):
+                        @pl.when(valid)
+                        def _():
+                            take(zi, q)
+                    if t == last:
+                        part += prune(q, cut)
+                        out_copy(q).start()
+    if last <= half:
+        cut = cuts()
         for q in range(chunks):
-            step(t, q)
-            if t > half:
-                for valid, zi in sides(t):
-                    @pl.when(valid)
-                    def _():
-                        take(zi, q)
-        if t == half:
-            bulk(t)
-
-    def all_sum(phase, part):
-        sums[phase, 0] = part
-
-        def sum_copy(d):
-            return pltpu.make_async_remote_copy(
-                src_ref=sums.at[phase, 0], dst_ref=sums.at[phase, d],
-                send_sem=sum_send.at[phase, d], recv_sem=sum_recv.at[phase, d],
-                device_id={"row": (me_row + d) % row_dev},
-            )
-
-        for d in range(1, row_dev):
-            sum_copy(d).start()
-        total = part
-        for d in range(1, row_dev):
-            sum_copy(d).wait()
-            total = total + sums[phase, d]
-        return total
-
-    cut = (
-        0.125 * thr_ref[...].astype(jnp.float32)
-        * (all_sum(0, jnp.sum(acc[...], axis=0, keepdims=True)) / order)
-    )
-    parts = []
-    for b in range(cols // TB):
-        c = slice(b * TB, (b + 1) * TB)
-        part = jnp.zeros((1, TB), jnp.float32)
-        for a in range(rows // TB):
-            r = slice(a * TB, (a + 1) * TB)
-            pruned = jnp.maximum(acc[r, c] - cut[:, c], 0.0) * keep_ref[a, b].astype(jnp.float32)
-            acc[r, c] = pruned
-            part += jnp.sum(pruned, axis=0, keepdims=True)
-        parts.append(part)
-    totals = all_sum(1, jnp.concatenate(parts, axis=1)) / order
-    out_ref[...] = (acc[...] * (1.0 / jnp.maximum(totals, 0.1))).astype(jnp.bfloat16)
+            part += prune(q, cut)
+            out_copy(q).start()
+
+    sums[0] = part
+
+    def sum_copy(d):
+        return pltpu.make_async_remote_copy(
+            src_ref=sums.at[0], dst_ref=sums.at[d],
+            send_sem=sum_send.at[d], recv_sem=sum_recv.at[d],
+            device_id={"row": (me_row + d) % row_dev},
+        )
+
+    for d in range(1, row_dev):
+        sum_copy(d).start()
+    for d in range(1, row_dev):
+        sum_copy(d).wait()
+        part += sums[d]
+    totals_ref[...] = 1.0 / jnp.maximum(part / order, 0.1)
+
+    for q in range(chunks):
+        out_copy(q).wait()
 
     for q in range(chunks):
         for zi in range(chips):
@@ -226,34 +284,38 @@
     width = max(w for w in range(1, row_dev + 1) if row_dev % w == 0 and w * w <= row_dev)
     chips = col_dev // CORES
     dma = pltpu.SemaphoreType.DMA
-    return pl.pallas_call(
+    vmem = pl.BlockSpec(memory_space=pltpu.VMEM)
+    pruned, scale = pl.pallas_call(
         functools.partial(kernel, row_dev, col_dev, width, CHUNKS, rows * row_dev),
-        out_shape=jax.ShapeDtypeStruct((rows, cols), jnp.bfloat16),
-        in_specs=[
-            pl.BlockSpec(memory_space=pltpu.VMEM),
-            pl.BlockSpec(memory_space=pltpu.SMEM),
-            pl.BlockSpec(memory_space=pltpu.SMEM),
-            pl.BlockSpec(memory_space=pltpu.VMEM),
-        ],
-        out_specs=pl.BlockSpec(memory_space=pltpu.VMEM),
+        out_shape=(
+            jax.ShapeDtypeStruct((rows, cols), jnp.float32),
+            jax.ShapeDtypeStruct((1, cols), jnp.float32),
+        ),
+        in_specs=[vmem] * 4,
+        out_specs=(pl.BlockSpec(memory_space=pl.ANY), vmem),
         scratch_shapes=[
             pltpu.VMEM((col_dev, rows, cols), jnp.bfloat16),
             pltpu.VMEM((row_dev * rows, cols), jnp.bfloat16),
             pltpu.VMEM((rows, cols), jnp.float32),
-            pltpu.VMEM((2, row_dev, 1, cols), jnp.float32),
+            pltpu.VMEM((row_dev, 1, cols), jnp.float32),
+            pltpu.VMEM((col_dev, 1, cols), jnp.float32),
             dma((2, chips, CHUNKS)),
             dma((chips, CHUNKS)),
             dma((chips, CHUNKS)),
             dma((chips, CHUNKS)),
             dma((2, row_dev, CHUNKS)),
             dma((row_dev, CHUNKS)),
-            dma((2, row_dev)),
-            dma((2, row_dev)),
+            dma((row_dev,)),
+            dma((row_dev,)),
+            dma((col_dev,)),
+            dma((col_dev,)),
+            dma((CHUNKS,)),
         ],
         compiler_params=pltpu.CompilerParams(
             collective_id=0, has_side_effects=True, vmem_limit_bytes=60 * 1024 * 1024
         ),
-    )(values, tile_mask, keep_mask, thr_index.reshape(1, cols))
+    )(values, tile_mask.T, keep_mask.T, thr_index.reshape(1, cols))
+    return (pruned * scale).astype(jnp.bfloat16)
 
 
 def solution(mesh):

time: 88.7 us -> 86.8 us (0.979)
  local copies, waits for them, and re-layouts: 4.3 us -> 0 us
  other arithmetic: 0 us -> 2.84 us
    unnamed x5 -> x0, local copies, waits for them, and re-layouts: 4.3 us -> none
    convert_element_type x0 -> x1, other arithmetic: none -> 2.84 us  [on_device(): return (pruned * scale).astype(jnp.bfloat16)]
where the time goes in v2:
time: 86.8 us; the launch traced here: 86.6 us
  Pallas kernels  83.8 us (97%)
  other arithmetic  2.84 us (3%)
    pallas_call x1, Pallas kernels, on_device(): pl.pallas_call(functools.partial(kernel, row_dev, col_dev, width, CHUNKS,...  83.8 us
    convert_element_type x1, other arithmetic, on_device(): return (pruned * scale).astype(jnp.bfloat16)  2.84 us

profile of v2, /device:TPU:0, one launch (start us, length us, event | category | flops | bytes accessed | tf_op | source)
XLA Modules:
  0.0 86.6 jit_solution(14201875818253206369)
XLA Ops:
  0.0 83.8 %shard_map.46 = (f32[1024,512]{1,0:T(8,128)}, f32[1,512]{1,0:T(1,128)}) custom-call(bf16[1024,512]{1,0:T(8,128)(2,1)} %v_ref.1, s32[4,8]{1,0:T(4,128)} %bitcast.4, s32[4,8]{1,0:T(4,128)} %bitcast.5, s32[1,512]{1,0:T(1,128)} %bitcast.6), custom_call_target="tpu_custom_call" | custom-call | tf_op jit(solution)/shard_map/pallas_call | solution.py:288
  83.8 2.8 %multiply_convert_fusion = bf16[1024,512]{1,0:T(8,128)(2,1)} fusion(f32[1024,512]{1,0:T(8,128)} %get-tuple-element.7, f32[512]{0:T(512)} %bitcast.7), kind=kLoop, calls=%fused_computation | loop fusion | flops 1048576 | bytes 3147776 | tf_op jit(solution)/shard_map/convert_element_type | solution.py:318

commit v3 on v2

--- a/solution.py
+++ b/solution.py
@@ -22,7 +22,7 @@
     v_ref, tile_ref, keep_ref, thr_ref, pruned_ref, totals_ref,
     row_panel, col_panel, acc, sums, stats,
     line_send, line_recv, pair_send, pair_recv, ring_send, ring_recv,
-    sum_send, sum_recv, stat_send, stat_recv, out_sem,
+    sum_send, sum_recv, stat_send, stat_recv, out_sem, loaded, load_sem, token,
 ):
     rows, cols = v_ref.shape
     step_rows = rows // chunks
@@ -36,22 +36,41 @@
         return snake((pos + offset + row_dev) % row_dev, width)
 
     barrier = pltpu.get_barrier_semaphore()
-    for d in range(1, row_dev):
-        pl.semaphore_signal(barrier, inc=1, device_id={"row": (me_row + d) % row_dev})
-    for d in range(1, col_dev):
-        pl.semaphore_signal(barrier, inc=1, device_id={"col": (me_col + d) % col_dev})
+    pl.semaphore_signal(barrier, inc=1, device_id={"col": z * CORES + 1 - core})
+    peers = 1 + (z > 0).astype(jnp.int32) + (z < chips - 1).astype(jnp.int32)
+    for offset in ((1, -1) if row_dev > 2 else (1,) * half):
+        pl.semaphore_signal(barrier, inc=1, device_id={"row": ring_device(offset)})
+        peers += 1
+
+    @pl.when(z > 0)
+    def _():
+        pl.semaphore_signal(barrier, inc=1, device_id={"col": me_col - CORES})
+
+    @pl.when(z < chips - 1)
+    def _():
+        pl.semaphore_signal(barrier, inc=1, device_id={"col": me_col + CORES})
+
+    def load(q):
+        spot = pl.ds(q * step_rows, step_rows)
+        return pltpu.make_async_copy(v_ref.at[spot], loaded.at[spot], load_sem.at[q])
+
+    for q in range(chunks):
+        load(q).start()
 
     stored = tile_ref[...].astype(jnp.float32)
     kept = keep_ref[...].astype(jnp.float32)
-    for a in range(rows // TB):
+    height = min(step_rows, TB)
+    for lo in range(0, rows, height):
+        if lo % step_rows == 0:
+            load(lo // step_rows).wait()
         for b in range(cols // TB):
-            r, c = slice(a * TB, (a + 1) * TB), slice(b * TB, (b + 1) * TB)
-            scale = jnp.broadcast_to(stored[b : b + 1, a : a + 1], (TB, TB))
-            tile = (v_ref[r, c].astype(jnp.float32) * scale).astype(jnp.bfloat16)
+            r, c = slice(lo, lo + height), slice(b * TB, (b + 1) * TB)
+            scale = jnp.broadcast_to(stored[b : b + 1, lo // TB : lo // TB + 1], (height, TB))
+            tile = (loaded[r, c].astype(jnp.float32) * scale).astype(jnp.bfloat16)
             row_panel[me_col, r, c] = tile
-            col_panel[pl.ds(pl.multiple_of(me_row * rows + a * TB, TB), TB), c] = tile
-
-    pl.semaphore_wait(barrier, row_dev + col_dev - 2)
+            col_panel[pl.ds(pl.multiple_of(me_row * rows + lo, height), height), c] = tile
+
+    pl.semaphore_wait(barrier, peers)
 
     def row_part(block, q):
         return row_panel.at[block, pl.ds(q * step_rows, step_rows)]
@@ -101,6 +120,20 @@
             if on_ring(1, q, to_right):
                 ring_copy(me_row, q, to_right).start()
         pair_copy(z, q, core).start()
+
+    for to_right in (1, 0):
+        first, end = (0, chips - 1) if to_right else (chips - 1, 0)
+
+        @pl.when(z != first)
+        def _():
+            pl.semaphore_wait(token.at[to_right], 1)
+
+        @pl.when(z != end)
+        def _():
+            pl.semaphore_signal(
+                token.at[to_right], inc=1,
+                device_id={"col": me_col + (CORES if to_right else -CORES)},
+            )
 
     def line_step(t, q):
         for to_right in (1, 0):
@@ -291,7 +324,7 @@
             jax.ShapeDtypeStruct((rows, cols), jnp.float32),
             jax.ShapeDtypeStruct((1, cols), jnp.float32),
         ),
-        in_specs=[vmem] * 4,
+        in_specs=[pl.BlockSpec(memory_space=pl.ANY)] + [vmem] * 3,
         out_specs=(pl.BlockSpec(memory_space=pl.ANY), vmem),
         scratch_shapes=[
             pltpu.VMEM((col_dev, rows, cols), jnp.bfloat16),
@@ -310,6 +343,9 @@
             dma((col_dev,)),
             dma((col_dev,)),
             dma((CHUNKS,)),
+            pltpu.VMEM((rows, cols), jnp.bfloat16),
+            dma((CHUNKS,)),
+            pltpu.SemaphoreType.REGULAR((2,)),
         ],
         compiler_params=pltpu.CompilerParams(
             collective_id=0, has_side_effects=True, vmem_limit_bytes=60 * 1024 * 1024

time: 86.8 us -> 85.7 us (0.987)
  Pallas kernels: 83.8 us -> 82.7 us
    pallas_call x1, Pallas kernels: 83.8 us -> 82.7 us  [on_device(): pl.pallas_call(functools.partial(kernel, row_dev, col_dev, width, CHUNKS,...]
where the time goes in v3:
time: 85.7 us; the launch traced here: 85.6 us
  Pallas kernels  82.7 us (96%)
  other arithmetic  2.84 us (3%)
    pallas_call x1, Pallas kernels, on_device(): pl.pallas_call(functools.partial(kernel, row_dev, col_dev, width, CHUNKS,...  82.7 us
    convert_element_type x1, other arithmetic, on_device(): return (pruned * scale).astype(jnp.bfloat16)  2.84 us

profile of v3, /device:TPU:0, one launch (start us, length us, event | category | flops | bytes accessed | tf_op | source)
XLA Modules:
  0.0 85.6 jit_solution(15926954886684788424)
XLA Ops:
  0.0 82.7 %shard_map.46 = (f32[1024,512]{1,0:T(8,128)}, f32[1,512]{1,0:T(1,128)}) custom-call(bf16[1024,512]{1,0:T(8,128)(2,1)} %v_ref.1, s32[4,8]{1,0:T(4,128)} %bitcast.4, s32[4,8]{1,0:T(4,128)} %bitcast.5, s32[1,512]{1,0:T(1,128)} %bitcast.6), custom_call_target="tpu_custom_call" | custom-call | tf_op jit(solution)/shard_map/pallas_call | solution.py:321
  82.7 2.8 %multiply_convert_fusion = bf16[1024,512]{1,0:T(8,128)(2,1)} fusion(f32[1024,512]{1,0:T(8,128)} %get-tuple-element.7, f32[512]{0:T(512)} %bitcast.7), kind=kLoop, calls=%fused_computation | loop fusion | flops 1048576 | bytes 3147776 | tf_op jit(solution)/shard_map/convert_element_type | solution.py:354

commit v4 on v3

--- a/solution.py
+++ b/solution.py
@@ -19,10 +19,10 @@
 
 def kernel(
     row_dev, col_dev, width, chunks, order,
-    v_ref, tile_ref, keep_ref, thr_ref, pruned_ref, totals_ref,
-    row_panel, col_panel, acc, sums, stats,
+    v_ref, tile_ref, keep_ref, thr_ref, acc, totals_ref,
+    row_panel, col_panel, sums, stats,
     line_send, line_recv, pair_send, pair_recv, ring_send, ring_recv,
-    sum_send, sum_recv, stat_send, stat_recv, out_sem, loaded, load_sem, token,
+    sum_send, sum_recv, stat_send, stat_recv, loaded, load_sem, token,
 ):
     rows, cols = v_ref.shape
     step_rows = rows // chunks
@@ -219,10 +219,6 @@
                     @pl.when(valid)
                     def _():
                         take(zi, q)
-
-    def out_copy(q):
-        spot = pl.ds(q * step_rows, step_rows)
-        return pltpu.make_async_copy(acc.at[spot], pruned_ref.at[spot], out_sem.at[q])
 
     def prune(q, cut):
         parts = []
@@ -268,12 +264,10 @@
                             take(zi, q)
                     if t == last:
                         part += prune(q, cut)
-                        out_copy(q).start()
     if last <= half:
         cut = cuts()
         for q in range(chunks):
             part += prune(q, cut)
-            out_copy(q).start()
 
     sums[0] = part
 
@@ -290,9 +284,6 @@
         sum_copy(d).wait()
         part += sums[d]
     totals_ref[...] = 1.0 / jnp.maximum(part / order, 0.1)
-
-    for q in range(chunks):
-        out_copy(q).wait()
 
     for q in range(chunks):
         for zi in range(chips):
@@ -321,15 +312,14 @@
     pruned, scale = pl.pallas_call(
         functools.partial(kernel, row_dev, col_dev, width, CHUNKS, rows * row_dev),
         out_shape=(
-            jax.ShapeDtypeStruct((rows, cols), jnp.float32),
+            pltpu.VMEM((rows, cols), jnp.float32),
             jax.ShapeDtypeStruct((1, cols), jnp.float32),
         ),
         in_specs=[pl.BlockSpec(memory_space=pl.ANY)] + [vmem] * 3,
-        out_specs=(pl.BlockSpec(memory_space=pl.ANY), vmem),
+        out_specs=(vmem, vmem),
         scratch_shapes=[
             pltpu.VMEM((col_dev, rows, cols), jnp.bfloat16),
             pltpu.VMEM((row_dev * rows, cols), jnp.bfloat16),
-            pltpu.VMEM((rows, cols), jnp.float32),
             pltpu.VMEM((row_dev, 1, cols), jnp.float32),
             pltpu.VMEM((col_dev, 1, cols), jnp.float32),
             dma((2, chips, CHUNKS)),
@@ -342,13 +332,13 @@
             dma((row_dev,)),
             dma((col_dev,)),
             dma((col_dev,)),
-            dma((CHUNKS,)),
             pltpu.VMEM((rows, cols), jnp.bfloat16),
             dma((CHUNKS,)),
             pltpu.SemaphoreType.REGULAR((2,)),
         ],
         compiler_params=pltpu.CompilerParams(
-            collective_id=0, has_side_effects=True, vmem_limit_bytes=60 * 1024 * 1024
+            collective_id=0, has_side_effects=True,
+            vmem_limit_bytes=63 * 2**20 - 4 * rows * cols + 2**19,
         ),
     )(values, tile_mask.T, keep_mask.T, thr_index.reshape(1, cols))
     return (pruned * scale).astype(jnp.bfloat16)

time: 85.7 us -> 84.7 us (0.988)
  other arithmetic: 2.84 us -> 1.92 us
    convert_element_type x1, other arithmetic: 2.84 us -> 1.92 us  [on_device(): return (pruned * scale).astype(jnp.bfloat16)]
where the time goes in v4:
time: 84.7 us; the launch traced here: 84.6 us
  Pallas kernels  82.6 us (98%)
  other arithmetic  1.92 us (2%)
    pallas_call x1, Pallas kernels, on_device(): pl.pallas_call(functools.partial(kernel, row_dev, col_dev, width, CHUNKS,...  82.6 us
    convert_element_type x1, other arithmetic, on_device(): return (pruned * scale).astype(jnp.bfloat16)  1.92 us

profile of v4, /device:TPU:0, one launch (start us, length us, event | category | flops | bytes accessed | tf_op | source)
XLA Modules:
  0.0 84.6 jit_solution(12793286102589741739)
XLA Ops:
  0.0 82.6 %shard_map.46 = (f32[1024,512]{1,0:T(8,128)S(1)}, f32[1,512]{1,0:T(1,128)}) custom-call(bf16[1024,512]{1,0:T(8,128)(2,1)} %v_ref.1, s32[4,8]{1,0:T(4,128)} %bitcast.4, s32[4,8]{1,0:T(4,128)} %bitcast.5, s32[1,512]{1,0:T(1,128)} %bitcast.6), custom_call_target="tpu_custom_call" | custom-call | tf_op jit(solution)/shard_map/pallas_call | solution.py:312
  82.6 1.9 %multiply_convert_fusion = bf16[1024,512]{1,0:T(8,128)(2,1)} fusion(f32[1024,512]{1,0:T(8,128)S(1)} %get-tuple-element.7, f32[512]{0:T(512)} %bitcast.7), kind=kLoop, calls=%fused_computation | loop fusion | flops 1048576 | bytes 3147776 | tf_op jit(solution)/shard_map/convert_element_type | solution.py:344

commit v5 on v4

--- a/solution.py
+++ b/solution.py
@@ -9,7 +9,7 @@
 
 TB = 128
 CORES = 2
-CHUNKS = 8
+CHUNKS = 16
 
 
 def snake(index, width):

time: 84.7 us -> 103 us (1.22)
  Pallas kernels: 82.6 us -> 101 us
    pallas_call x1, Pallas kernels: 82.6 us -> 101 us  [on_device(): pl.pallas_call(functools.partial(kernel, row_dev, col_dev, width, CHUNKS,...]
where the time goes in v5:
time: 103 us
  Pallas kernels  101 us (98%)
  other arithmetic  1.92 us (2%)
    pallas_call x1, Pallas kernels, on_device(): pl.pallas_call(functools.partial(kernel, row_dev, col_dev, width, CHUNKS,...  101 us

profile of v5, /device:TPU:0, one launch (start us, length us, event | category | flops | bytes accessed | tf_op | source)
XLA Modules:
  0.0 102.6 jit_solution(9317081849157519807)
XLA Ops:
  0.0 100.6 %shard_map.46 = (f32[1024,512]{1,0:T(8,128)S(1)}, f32[1,512]{1,0:T(1,128)}) custom-call(bf16[1024,512]{1,0:T(8,128)(2,1)} %v_ref.1, s32[4,8]{1,0:T(4,128)} %bitcast.4, s32[4,8]{1,0:T(4,128)} %bitcast.5, s32[1,512]{1,0:T(1,128)} %bitcast.6), custom_call_target="tpu_custom_call" | custom-call | tf_op jit(solution)/shard_map/pallas_call | solution.py:312
  100.6 1.9 %multiply_convert_fusion = bf16[1024,512]{1,0:T(8,128)(2,1)} fusion(f32[1024,512]{1,0:T(8,128)S(1)} %get-tuple-element.7, f32[512]{0:T(512)} %bitcast.7), kind=kLoop, calls=%fused_computation | loop fusion | flops 1048576 | bytes 3147776 | tf_op jit(solution)/shard_map/convert_element_type | solution.py:344
